TPU v7x, 256 devices: a whole 4x4x8 slice. The times are simulated.
256 devices in a mesh: shard: 64 (over z, x, core), model: 4 (over y).
Axes of the slice: x: 4, y: 4, z: 8, core: 2. Of those that a mesh axis runs over, the one named last changes fastest.
Arguments:
- grad_stack: float32 [512, 128, 2048], P(None, 'shard', 'model'), may hold values from -6 to 6
- moment_stack: float32 [512, 128, 2048], P(None, 'shard', 'model'), may hold values from -6 to 6
- weight_stack: float32 [512, 128, 2048], P(None, 'shard', 'model'), may hold values from -0.1875 to 0.1875
Outputs:
- new_weights: float32 [512, 128, 2048], P(None, 'shard', 'model')
- new_momentum: float32 [512, 128, 2048], P(None, 'shard', 'model')
All inputs are finite; a program needn't handle non-finite values.
Results may differ from a plain program's by a relative error of at most 0.00021.
Values sent between devices are 32-bit elements; how exact they have to be, the bound alone decides.
A program may use at most 64 MiB of HBM per device.

v0:
```python
import jax
import jax.numpy as jnp
from jax import lax
from jax.sharding import PartitionSpec as P

hold_rate = 0.95
learn_rate = 1.0
decay_rate = 0.1
HIGH = lax.Precision.HIGHEST


def mul(a, b):
    return jnp.einsum("mij,mjk->mik", a, b, precision=HIGH)


def chain(gram, steps):
    eye = jnp.eye(gram.shape[-1], dtype=gram.dtype)
    total = None
    for step in range(steps):
        factor = 3.4445 * eye - 4.775 * gram + 2.0315 * mul(gram, gram)
        total = factor if total is None else mul(factor, total)
        if step < steps - 1:
            gram = mul(mul(factor, gram), factor)
    return total


def summed_gram(rows):
    part = jnp.einsum("mik,mjk->mij", rows, rows, precision=HIGH)
    parts = lax.all_to_all(part, "model", split_axis=0, concat_axis=0, tiled=True)
    return parts.reshape(4, -1, *parts.shape[1:]).sum(axis=0)


def on_device(grad_stack, moment_stack, weight_stack):
    new_momentum = hold_rate * moment_stack + grad_stack
    rows = lax.all_to_all(new_momentum, "shard", split_axis=0, concat_axis=1, tiled=True)
    gram = summed_gram(rows)
    scale = lax.rsqrt(jnp.trace(gram, axis1=1, axis2=2)[:, None, None] + 1e-06)
    first = chain(gram * scale * scale, 2) * scale
    rows = mul(lax.all_gather(first, "model", axis=0, tiled=True), rows)
    second = chain(summed_gram(rows), 3)
    rows = mul(lax.all_gather(second, "model", axis=0, tiled=True), rows)
    back = lax.all_to_all(rows, "shard", split_axis=1, concat_axis=0, tiled=True)
    new_weights = (1.0 - learn_rate * decay_rate) * weight_stack - learn_rate * back
    return (new_weights, new_momentum)


def solution(mesh):
    spec = P(None, "shard", "model")
    return jax.shard_map(
        on_device, mesh=mesh, in_specs=(spec,) * 3, out_specs=(spec,) * 2, check_vma=False
    )
```

profile of v0, /device:TPU:2, one launch (start us, length us, event | category | flops | bytes accessed | tf_op | source)
XLA Modules:
  0.0 198.5 jit_solution(3235271127646908158)
XLA Ops:
  0.6 3.7 %multiply_add_fusion = f32[512,2,512]{2,1,0:T(2,128)S(1)} fusion(f32[512,2,512]{2,1,0:T(2,128)} %param.3, f32[512,2,512]{2,1,0:T(2,128)} %param.4), kind=kLoop, calls=%fused_computation.2 | loop fusion | flops 1048576 | bytes 6291456 | tf_op jit(solution)/shard_map/add | solution.py:34
  4.3 0.0 copy-start.2
  4.3 63.1 %all_to_all.46 = f32[512,2,512]{2,1,0:T(2,128)S(1)} all-to-all(f32[512,2,512]{2,1,0:T(2,128)S(1)} %multiply_add_fusion), channel_id=1, replica_groups=mesh['shard'=64,'model'=4] {'shard'}, dimensions={0} | all-to-all | bytes 4194304 | tf_op jit(solution)/shard_map/all_to_all | solution.py:35
  67.4 0.0 copy-done.2
  67.4 2.1 %copy.11 = f32[64,8,2,512]{3,2,0,1:T(2,128)} copy(f32[64,8,2,512]{3,2,1,0:T(2,128)S(1)} %bitcast.46) | data formatting | bytes 4194304 | tf_op jit(solution)/shard_map/all_to_all | solution.py:35
  69.4 2.7 %all_to_all.35 = f32[8,128,512]{2,1,0:T(8,128)S(1)} reshape(f32[8,64,2,512]{3,2,1,0:T(2,128)} %bitcast.44) | data formatting | bytes 4194304 | tf_op jit(solution)/shard_map/all_to_all | solution.py:35
  72.1 2.9 %fusion.8 = f32[8,128,128]{2,1,0:T(8,128)} fusion(f32[8,128,512]{2,1,0:T(8,128)S(1)} %all_to_all.35), kind=kOutput, calls=%fused_computation.22 | convolution fusion | flops 805306368 | bytes 2621440 | tf_op jit(solution)/shard_map/mik,mjk->mij/dot_general | solution.py:28
  75.0 4.5 %all-to-all-start.1 = ((f32[8,128,128]{2,1,0:T(8,128)}), f32[8,128,128]{2,1,0:T(8,128)S(1)}, u32[]{:S(2)}, u32[]{:S(2)}) async-start(f32[8,128,128]{2,1,0:T(8,128)} %fusion.8), calls=%async_computation.1 | async-start | bytes 1048576 | tf_op jit(solution)/shard_map/all_to_all | solution.py:29
  79.5 8.0 %all-to-all-done.1 = f32[8,128,128]{2,1,0:T(8,128)S(1)} async-done(((f32[8,128,128]{2,1,0:T(8,128)}), f32[8,128,128]{2,1,0:T(8,128)S(1)}, u32[]{:S(2)}, u32[]{:S(2)}) %all-to-all-start.1) | async-done | bytes 524320 | tf_op jit(solution)/shard_map/all_to_all | solution.py:29
  87.6 0.1 select_reduce_fusion
  87.7 0.4 fusion.4
  88.1 0.3 fusion.5
  88.4 0.3 fusion.9
  88.7 0.3 fusion.3
  89.0 0.3 convolution_multiply_fusion.3
  89.2 12.8 %all_gather.6 = f32[8,128,128]{2,1,0:T(8,128)S(1)} all-gather(f32[2,128,128]{2,1,0:T(8,128)S(1)} %convolution_multiply_fusion.3), channel_id=1, replica_groups=mesh['shard'=64,'model'=4] {'model'}, dimensions={0}, use_global_device_ids=true | all-gather | bytes 655360 | tf_op jit(solution)/shard_map/all_gather | solution.py:39
  102.0 1.8 fusion.10
  103.9 0.0 copy-start
  103.9 2.1 %fusion.11 = f32[8,128,128]{2,1,0:T(8,128)S(1)} fusion(f32[8,128,512]{2,1,0:T(8,128)S(1)} %fusion.10), kind=kOutput, calls=%fused_computation.25 | convolution fusion | flops 805306368 | bytes 2621440 | tf_op jit(solution)/shard_map/mik,mjk->mij/dot_general | solution.py:28
  106.0 0.0 copy-done
  106.0 11.3 %all_to_all.47 = f32[8,128,128]{2,1,0:T(8,128)S(1)} all-to-all(f32[8,128,128]{2,1,0:T(8,128)S(1)} %fusion.11), channel_id=1, replica_groups=mesh['shard'=64,'model'=4] {'model'}, dimensions={0} | all-to-all | bytes 1048576 | tf_op jit(solution)/shard_map/all_to_all | solution.py:29
  117.3 0.0 copy-start.1
  117.4 0.3 fusion.2
  117.6 0.3 fusion.12
  117.9 0.3 fusion.13
  118.2 0.3 fusion.1
  118.5 0.3 fusion.16
  118.7 0.3 fusion.14
  119.0 0.3 fusion.15
  119.3 0.3 fusion
  119.6 0.3 fusion.17
  119.8 12.8 %all_gather.7 = f32[8,128,128]{2,1,0:T(8,128)S(1)} all-gather(f32[2,128,128]{2,1,0:T(8,128)S(1)} %fusion.17), channel_id=1, replica_groups=mesh['shard'=64,'model'=4] {'model'}, dimensions={0}, use_global_device_ids=true | all-gather | bytes 655360 | tf_op jit(solution)/shard_map/all_gather | solution.py:41
  132.6 0.0 copy-done.1
  132.6 1.8 fusion.18
  134.5 1.2 copy.8
  135.7 57.6 %all_to_all.48 = f32[8,128,512]{2,0,1:T(8,128)S(1)} all-to-all(f32[8,128,512]{2,0,1:T(8,128)S(1)} %copy.8), channel_id=1, replica_groups=mesh['shard'=64,'model'=4] {'shard'}, dimensions={1} | all-to-all | bytes 4194304 | tf_op jit(solution)/shard_map/all_to_all | solution.py:42
  193.3 0.0 copy-start.3
  193.3 1.9 copy.9
  195.3 0.0 copy-done.3
  195.3 3.3 %bitcast_subtract_fusion = f32[512,2,512]{2,1,0:T(2,128)} fusion(f32[64,8,2,512]{3,2,1,0:T(2,128)S(1)} %copy.9, f32[512,2,512]{2,1,0:T(2,128)S(1)} %copy-done.3), kind=kLoop, calls=%fused_computation | loop fusion | flops 1048576 | bytes 6291456 | tf_op jit(solution)/shard_map/sub | solution.py:43
  (5 shorter events, 0.1 us)
Async XLA Ops:
  4.3 63.1 %copy-start.2 = (f32[512,2,512]{2,1,0:T(2,128)}, f32[512,2,512]{2,1,0:T(2,128)S(1)}, u32[]{:S(2)}) copy-start(f32[512,2,512]{2,1,0:T(2,128)S(1)} %multiply_add_fusion) | copy-start | bytes 6291460
  75.0 12.5 %all-to-all-start.1 = ((f32[8,128,128]{2,1,0:T(8,128)}), f32[8,128,128]{2,1,0:T(8,128)S(1)}, u32[]{:S(2)}, u32[]{:S(2)}) async-start(f32[8,128,128]{2,1,0:T(8,128)} %fusion.8), calls=%async_computation.1 | async-start | bytes 1048576 | tf_op jit(solution)/shard_map/all_to_all | solution.py:29
  103.9 2.1 %copy-start = (f32[8,128,512]{2,1,0:T(8,128)}, f32[8,128,512]{2,1,0:T(8,128)S(1)}, u32[]{:S(2)}) copy-start(f32[8,128,512]{2,1,0:T(8,128)S(1)} %fusion.10) | copy-start | bytes 6291460
  117.3 15.3 %copy-start.1 = (f32[8,128,512]{2,1,0:T(8,128)S(1)}, f32[8,128,512]{2,1,0:T(8,128)}, u32[]{:S(2)}) copy-start(f32[8,128,512]{2,1,0:T(8,128)} %copy-done) | copy-start | bytes 6291460
  193.3 1.9 copy-start.3
where the time goes:
time: 199 us
  blocking collectives  158 us (79%)
  matrix products  12.5 us (6%)
  waiting for transfers between devices  8.05 us (4%)
  local copies, waits for them, and re-layouts  7.95 us (4%)
  other arithmetic  7.12 us (4%)
  starting transfers between devices  4.46 us (2%)
    all_to_all x1, blocking collectives, on_device(): lax.all_to_all(new_momentum, 'shard', split_axis=0, concat_axis=1, tiled=...  63.1 us
    all_to_all x1, blocking collectives, on_device(): lax.all_to_all(rows, 'shard', split_axis=1, concat_axis=0, tiled=True)  57.6 us
    all_gather x1, blocking collectives, on_device(): rows = mul(lax.all_gather(first, 'model', axis=0, tiled=True), rows)  12.8 us
    all_gather x1, blocking collectives, on_device(): rows = mul(lax.all_gather(second, 'model', axis=0, tiled=True), rows)  12.8 us
    all_to_all x1, blocking collectives, summed_gram(): lax.all_to_all(part, 'model', split_axis=0, concat_axis=0, tiled=True)  11.3 us
    all_to_all x1, waiting for transfers between devices, summed_gram(): lax.all_to_all(part, 'model', split_axis=0, concat_axis=0, tiled=True)  8.05 us
    dot_general x16, matrix products, mul(): return jnp.einsum('mij,mjk->mik', a, b, precision=HIGH)  7.6 us
    dot_general x2, matrix products, summed_gram(): part = jnp.einsum('mik,mjk->mij', rows, rows, precision=HIGH)  4.93 us
  transfers between devices with their start and end apart: 1, of which 1 were waited for; matrix products, arithmetic and copies ran while one was open for 0% of the time, Pallas kernels for 0%

commit v1 on v0

--- a/solution.py
+++ b/solution.py
@@ -7,6 +7,35 @@
 learn_rate = 1.0
 decay_rate = 0.1
 HIGH = lax.Precision.HIGHEST
+
+
+def pair_works(matrix):
+    bus_axis = "model"
+    formed, later, current_value = (
+        lax.axis_size(bus_axis),
+        lax.axis_index(bus_axis),
+        matrix.shape[0],
+    )
+    items = tuple((no * formed if kk == 0 else no for kk, no in enumerate(matrix.shape)))
+    parts_out = lax.dynamic_update_slice_in_dim(
+        jnp.zeros(items, matrix.dtype), matrix, later * current_value, axis=0
+    )
+    upper = new = matrix
+    for hop_no in range(1, formed // 2 + 1):
+        upper = lax.ppermute(
+            upper, bus_axis, tuple(((kk, (kk + 1) % formed) for kk in range(formed)))
+        )
+        parts_out = lax.dynamic_update_slice_in_dim(
+            parts_out, upper, (later - hop_no) % formed * current_value, axis=0
+        )
+        if 2 * hop_no < formed:
+            new = lax.ppermute(
+                new, bus_axis, tuple(((kk, (kk - 1) % formed) for kk in range(formed)))
+            )
+            parts_out = lax.dynamic_update_slice_in_dim(
+                parts_out, new, (later + hop_no) % formed * current_value, axis=0
+            )
+    return parts_out
 
 
 def mul(a, b):
@@ -38,7 +67,7 @@
     first = chain(gram * scale * scale, 2) * scale
     rows = mul(lax.all_gather(first, "model", axis=0, tiled=True), rows)
     second = chain(summed_gram(rows), 3)
-    rows = mul(lax.all_gather(second, "model", axis=0, tiled=True), rows)
+    rows = mul(pair_works(second), rows)
     back = lax.all_to_all(rows, "shard", split_axis=1, concat_axis=0, tiled=True)
     new_weights = (1.0 - learn_rate * decay_rate) * weight_stack - learn_rate * back
     return (new_weights, new_momentum)

time: 199 us -> 201 us (1.010)
  blocking collectives: 158 us -> 133 us
  waiting for transfers between devices: 8.05 us -> 26.3 us
  starting transfers between devices: 4.46 us -> 11.4 us
    all_gather x1 -> x0, blocking collectives: 12.8 us -> none  [on_device(): rows = mul(lax.all_gather(second, 'model', axis=0, tiled=True), rows)]
    all_to_all x1 -> x0, blocking collectives: 11.3 us -> none  [summed_gram(): lax.all_to_all(part, 'model', split_axis=0, concat_axis=0, tiled=True)]
    all_to_all x1 -> x2, waiting for transfers between devices: 8.05 us -> 17.2 us  [summed_gram(): lax.all_to_all(part, 'model', split_axis=0, concat_axis=0, tiled=True)]
    ppermute x0 -> x3, waiting for transfers between devices: none -> 9.07 us  [the longest x2 9.07 us: pair_works(): lax.ppermute(upper, bus_axis, tuple(((kk, (kk + 1) % formed) for kk in ra...]
    all_to_all x1 -> x2, starting transfers between devices: 4.46 us -> 8.12 us  [summed_gram(): lax.all_to_all(part, 'model', split_axis=0, concat_axis=0, tiled=True)]
    ppermute x0 -> x3, starting transfers between devices: none -> 3.31 us  [the longest x1 3.22 us: pair_works(): lax.ppermute(new, bus_axis, tuple(((kk, (kk - 1) % formed) for kk in rang...]
  transfers between devices with their start and end apart: 1 -> 5, of which waited for: 1 -> 4; matrix products, arithmetic and copies ran while one was open for 0% -> 0% of each run, Pallas kernels for 0% -> 0%
where the time goes in v1:
time: 201 us; the launch traced here: 200 us
  blocking collectives  133 us (66%)
  waiting for transfers between devices  26.3 us (13%)
  matrix products  13.3 us (7%)
  starting transfers between devices  11.4 us (6%)
  local copies, waits for them, and re-layouts  8.02 us (4%)
  other arithmetic  7.12 us (4%)
    all_to_all x1, blocking collectives, on_device(): lax.all_to_all(new_momentum, 'shard', split_axis=0, concat_axis=1, tiled=...  63.1 us
    all_to_all x1, blocking collectives, on_device(): lax.all_to_all(rows, 'shard', split_axis=1, concat_axis=0, tiled=True)  57.6 us
    all_to_all x2, waiting for transfers between devices, summed_gram(): lax.all_to_all(part, 'model', split_axis=0, concat_axis=0, tiled=True)  17.2 us
    all_gather x1, blocking collectives, on_device(): rows = mul(lax.all_gather(first, 'model', axis=0, tiled=True), rows)  12.8 us
    ppermute x2, waiting for transfers between devices, pair_works(): lax.ppermute(upper, bus_axis, tuple(((kk, (kk + 1) % formed) for kk in ra...  9.07 us
    all_to_all x2, starting transfers between devices, summed_gram(): lax.all_to_all(part, 'model', split_axis=0, concat_axis=0, tiled=True)  8.12 us
    dot_general x16, matrix products, mul(): return jnp.einsum('mij,mjk->mik', a, b, precision=HIGH)  7.57 us
    dot_general x2, matrix products, summed_gram(): part = jnp.einsum('mik,mjk->mij', rows, rows, precision=HIGH)  5.72 us
  transfers between devices with their start and end apart: 5, of which 4 were waited for; matrix products, arithmetic and copies ran while one was open for 0% of the time, Pallas kernels for 0%

profile of v1, /device:TPU:2, one launch (start us, length us, event | category | flops | bytes accessed | tf_op | source)
XLA Modules:
  0.0 200.5 jit_solution(3712491907873789845)
XLA Ops:
  0.6 3.7 %multiply_add_fusion = f32[512,2,512]{2,1,0:T(2,128)S(1)} fusion(f32[512,2,512]{2,1,0:T(2,128)} %param.3, f32[512,2,512]{2,1,0:T(2,128)} %param.4), kind=kLoop, calls=%fused_computation.2 | loop fusion | flops 1048576 | bytes 6291456 | tf_op jit(solution)/shard_map/add | solution.py:63
  4.3 0.0 copy-start.2
  4.3 63.1 %all_to_all.46 = f32[512,2,512]{2,1,0:T(2,128)S(1)} all-to-all(f32[512,2,512]{2,1,0:T(2,128)S(1)} %multiply_add_fusion), channel_id=1, replica_groups=mesh['shard'=64,'model'=4] {'shard'}, dimensions={0} | all-to-all | bytes 4194304 | tf_op jit(solution)/shard_map/all_to_all | solution.py:64
  67.4 0.0 copy-done.2
  67.4 2.1 %copy.11 = f32[64,8,2,512]{3,2,0,1:T(2,128)} copy(f32[64,8,2,512]{3,2,1,0:T(2,128)S(1)} %bitcast.46) | data formatting | bytes 4194304 | tf_op jit(solution)/shard_map/all_to_all | solution.py:64
  69.4 2.7 %all_to_all.35 = f32[8,128,512]{2,1,0:T(8,128)S(1)} reshape(f32[8,64,2,512]{3,2,1,0:T(2,128)} %bitcast.44) | data formatting | bytes 4194304 | tf_op jit(solution)/shard_map/all_to_all | solution.py:64
  72.1 0.0 copy-start
  72.2 2.9 %fusion.8 = f32[8,128,128]{2,1,0:T(8,128)} fusion(f32[8,128,512]{2,1,0:T(8,128)S(1)} %all_to_all.35), kind=kOutput, calls=%fused_computation.26 | convolution fusion | flops 805306368 | bytes 2621440 | tf_op jit(solution)/shard_map/mik,mjk->mij/dot_general | solution.py:57
  75.0 0.0 copy-done
  75.0 4.5 %all-to-all-start.1 = ((f32[8,128,128]{2,1,0:T(8,128)}), f32[8,128,128]{2,1,0:T(8,128)S(1)}, u32[]{:S(2)}, u32[]{:S(2)}) async-start(f32[8,128,128]{2,1,0:T(8,128)} %fusion.8), calls=%async_computation.1 | async-start | bytes 1048576 | tf_op jit(solution)/shard_map/all_to_all | solution.py:58
  79.5 8.0 %all-to-all-done.1 = f32[8,128,128]{2,1,0:T(8,128)S(1)} async-done(((f32[8,128,128]{2,1,0:T(8,128)}), f32[8,128,128]{2,1,0:T(8,128)S(1)}, u32[]{:S(2)}, u32[]{:S(2)}) %all-to-all-start.1) | async-done | bytes 524320 | tf_op jit(solution)/shard_map/all_to_all | solution.py:58
  87.6 0.0 copy-start.1
  87.6 0.1 select_reduce_fusion
  87.7 0.4 fusion.4
  88.1 0.3 fusion.5
  88.4 0.3 fusion.9
  88.7 0.3 fusion.3
  89.0 0.3 convolution_multiply_fusion.3
  89.3 12.8 %all_gather.3 = f32[8,128,128]{2,1,0:T(8,128)S(1)} all-gather(f32[2,128,128]{2,1,0:T(8,128)S(1)} %convolution_multiply_fusion.3), channel_id=1, replica_groups=mesh['shard'=64,'model'=4] {'model'}, dimensions={0}, use_global_device_ids=true | all-gather | bytes 655360 | tf_op jit(solution)/shard_map/all_gather | solution.py:68
  102.1 0.0 copy-done.1
  102.1 1.8 fusion.10
  103.9 2.9 %fusion.11 = f32[8,128,128]{2,1,0:T(8,128)} fusion(f32[8,128,512]{2,1,0:T(8,128)S(1)} %fusion.10), kind=kOutput, calls=%fused_computation.29 | convolution fusion | flops 805306368 | bytes 2621440 | tf_op jit(solution)/shard_map/mik,mjk->mij/dot_general | solution.py:57
  106.8 3.7 %all-to-all-start.2 = ((f32[8,128,128]{2,1,0:T(8,128)}), f32[8,128,128]{2,1,0:T(8,128)S(1)}, u32[]{:S(2)}, u32[]{:S(2)}) async-start(f32[8,128,128]{2,1,0:T(8,128)} %fusion.11), calls=%async_computation.2 | async-start | bytes 1048576 | tf_op jit(solution)/shard_map/all_to_all | solution.py:58
  110.4 9.2 %all-to-all-done.2 = f32[8,128,128]{2,1,0:T(8,128)S(1)} async-done(((f32[8,128,128]{2,1,0:T(8,128)}), f32[8,128,128]{2,1,0:T(8,128)S(1)}, u32[]{:S(2)}, u32[]{:S(2)}) %all-to-all-start.2) | async-done | bytes 524320 | tf_op jit(solution)/shard_map/all_to_all | solution.py:58
  119.6 0.3 fusion.2
  119.9 0.3 fusion.12
  120.2 0.3 fusion.13
  120.4 0.3 fusion.1
  120.7 0.3 fusion.16
  121.0 0.3 fusion.14
  121.3 0.3 fusion.15
  121.5 0.3 fusion
  121.9 0.3 constant_dynamic-update-slice_fusion.3
  122.1 0.1 collective-permute-start
  122.2 3.2 %collective-permute-start.1 = (f32[2,128,128]{2,1,0:T(8,128)S(1)}, f32[2,128,128]{2,1,0:T(8,128)S(1)}, u32[]{:S(2)}, u32[]{:S(2)}) collective-permute-start(f32[2,128,128]{2,1,0:T(8,128)S(1)} %get-tuple-element.3), channel_id=1, source_target_pairs={{0,3},{1,0},{2,1},{3,2},{4,7},{5,4},{6,5},{7,6},{8,11},{9,8},{10,9... | collective-permute-start | bytes 393224 | tf_op jit(solution)/shard_map/ppermute | solution.py:32
  125.5 2.9 %collective-permute-done = f32[2,128,128]{2,1,0:T(8,128)S(1)} collective-permute-done((f32[2,128,128]{2,1,0:T(8,128)S(1)}, f32[2,128,128]{2,1,0:T(8,128)S(1)}, u32[]{:S(2)}, u32[]{:S(2)}) %collective-permute-start) | collective-permute-done | bytes 131104 | tf_op jit(solution)/shard_map/ppermute | solution.py:25
  128.4 0.0 collective-permute-start.2
  128.4 0.0 collective-permute-done.1
  128.5 6.1 %collective-permute-done.2 = f32[2,128,128]{2,1,0:T(8,128)S(1)} collective-permute-done((f32[2,128,128]{2,1,0:T(8,128)S(1)}, f32[2,128,128]{2,1,0:T(8,128)S(1)}, u32[]{:S(2)}, u32[]{:S(2)}) %collective-permute-start.2) | collective-permute-done | bytes 131104 | tf_op jit(solution)/shard_map/ppermute | solution.py:25
  134.6 1.8 fusion.17
  136.4 1.2 copy.8
  137.7 57.6 %all_to_all.47 = f32[8,128,512]{2,0,1:T(8,128)S(1)} all-to-all(f32[8,128,512]{2,0,1:T(8,128)S(1)} %copy.8), channel_id=1, replica_groups=mesh['shard'=64,'model'=4] {'shard'}, dimensions={1} | all-to-all | bytes 4194304 | tf_op jit(solution)/shard_map/all_to_all | solution.py:71
  195.3 0.0 copy-start.3
  195.3 1.9 copy.9
  197.2 0.0 copy-done.3
  197.2 3.3 %bitcast_subtract_fusion = f32[512,2,512]{2,1,0:T(2,128)} fusion(f32[64,8,2,512]{3,2,1,0:T(2,128)S(1)} %copy.9, f32[512,2,512]{2,1,0:T(2,128)S(1)} %copy-done.3), kind=kLoop, calls=%fused_computation | loop fusion | flops 1048576 | bytes 6291456 | tf_op jit(solution)/shard_map/sub | solution.py:72
  (9 shorter events, 0.2 us)
Async XLA Ops:
  4.3 63.1 %copy-start.2 = (f32[512,2,512]{2,1,0:T(2,128)}, f32[512,2,512]{2,1,0:T(2,128)S(1)}, u32[]{:S(2)}) copy-start(f32[512,2,512]{2,1,0:T(2,128)S(1)} %multiply_add_fusion) | copy-start | bytes 6291460
  72.1 2.9 %copy-start = (f32[8,128,512]{2,1,0:T(8,128)}, f32[8,128,512]{2,1,0:T(8,128)S(1)}, u32[]{:S(2)}) copy-start(f32[8,128,512]{2,1,0:T(8,128)S(1)} %all_to_all.35) | copy-start | bytes 6291460
  75.0 12.5 %all-to-all-start.1 = ((f32[8,128,128]{2,1,0:T(8,128)}), f32[8,128,128]{2,1,0:T(8,128)S(1)}, u32[]{:S(2)}, u32[]{:S(2)}) async-start(f32[8,128,128]{2,1,0:T(8,128)} %fusion.8), calls=%async_computation.1 | async-start | bytes 1048576 | tf_op jit(solution)/shard_map/all_to_all | solution.py:58
  87.6 14.5 %copy-start.1 = (f32[8,128,512]{2,1,0:T(8,128)S(1)}, f32[8,128,512]{2,1,0:T(8,128)}, u32[]{:S(2)}) copy-start(f32[8,128,512]{2,1,0:T(8,128)} %copy-done) | copy-start | bytes 6291460
  106.8 12.8 %all-to-all-start.2 = ((f32[8,128,128]{2,1,0:T(8,128)}), f32[8,128,128]{2,1,0:T(8,128)S(1)}, u32[]{:S(2)}, u32[]{:S(2)}) async-start(f32[8,128,128]{2,1,0:T(8,128)} %fusion.11), calls=%async_computation.2 | async-start | bytes 1048576 | tf_op jit(solution)/shard_map/all_to_all | solution.py:58
  122.1 6.3 %collective-permute-start = (f32[2,128,128]{2,1,0:T(8,128)S(1)}, f32[2,128,128]{2,1,0:T(8,128)S(1)}, u32[]{:S(2)}, u32[]{:S(2)}) collective-permute-start(f32[2,128,128]{2,1,0:T(8,128)S(1)} %get-tuple-element.3), channel_id=1, source_target_pairs={{0,1},{1,2},{2,3},{3,0},{4,5},{5,6},{6,7},{7,4},{8,9},{9,10},{10,1... | collective-permute-start | bytes 393224 | tf_op jit(solution)/shard_map/ppermute | solution.py:25
  122.2 6.2 %collective-permute-start.1 = (f32[2,128,128]{2,1,0:T(8,128)S(1)}, f32[2,128,128]{2,1,0:T(8,128)S(1)}, u32[]{:S(2)}, u32[]{:S(2)}) collective-permute-start(f32[2,128,128]{2,1,0:T(8,128)S(1)} %get-tuple-element.3), channel_id=1, source_target_pairs={{0,3},{1,0},{2,1},{3,2},{4,7},{5,4},{6,5},{7,6},{8,11},{9,8},{10,9... | collective-permute-start | bytes 393224 | tf_op jit(solution)/shard_map/ppermute | solution.py:32
  128.4 6.2 %collective-permute-start.2 = (f32[2,128,128]{2,1,0:T(8,128)S(1)}, f32[2,128,128]{2,1,0:T(8,128)S(1)}, u32[]{:S(2)}, u32[]{:S(2)}) collective-permute-start(f32[2,128,128]{2,1,0:T(8,128)S(1)} %collective-permute-done), channel_id=1, source_target_pairs={{0,1},{1,2},{2,3},{3,0},{4,5},{5,6},{6,7},{7,4},{8,9},{9,10},{10,1... | collective-permute-start | bytes 393224 | tf_op jit(solution)/shard_map/ppermute | solution.py:25
  195.3 1.9 copy-start.3
